TPU v7x, 8 devices: a whole 2x2x1 slice. The times are simulated.
8 devices in a mesh: dp: 2 (over z, y), cp: 4 (over x, core).
Axes of the slice: x: 2, y: 2, z: 1, core: 2. Of those that a mesh axis runs over, the one named last changes fastest.
Arguments:
- x_in: bfloat16 [6, 1536, 2048], P('dp', 'cp'), parts along dimension 0
- positions: int32 [3072], P(('dp', 'cp')), parts along dimension 0
- long_factor: float32 [32], replicated
- norm_gain: float32 [2048], replicated
- w_qkv: bfloat16 [2048, 6144], replicated
- w_out: bfloat16 [2048, 2048], replicated
- grad_y: bfloat16 [6, 1536, 2048], P('dp', 'cp'), parts along dimension 0
Outputs:
- output 1: bfloat16 [6, 1536, 2048], P('dp', 'cp'), parts along dimension 0
- output 2: bfloat16 [6, 1536, 2048], P('dp', 'cp'), parts along dimension 0
- output 3: float32 [4096], P('dp'), parts along dimension 0
- output 4: float32 [4096, 6144], P('dp'), parts along dimension 0
- output 5: float32 [4096, 2048], P('dp'), parts along dimension 0
There are 2 independent parts. A program takes and returns all parts, laid end to end along the dimension named above; an argument that names none is the same for every part.
All inputs are finite; a program needn't handle non-finite values.
Results may differ from a plain program's by a relative error of at most 0.01427.
Values are sent between devices in bfloat16 or wider.
A program may use at most 1 GiB of HBM per device.

v0:
```python
import math
import jax
import jax.numpy as jnp
from jax import lax
from jax.sharding import PartitionSpec as P

NORM_EPS = 1e-5
MSCALE = math.sqrt(1.0 + math.log(32.0) / math.log(4096.0))
MASK_VALUE = -1e30


def rope_tables(positions, long_factor):
    half = long_factor.shape[0]
    exponent = jnp.arange(half, dtype=jnp.float32) * (1.0 / half)
    inv_freq = 1.0 / (long_factor * jnp.power(10000.0, exponent))
    angles = positions.astype(jnp.float32)[:, None] * inv_freq[None, :]
    angle_pair = jnp.concatenate([angles, angles], axis=-1)
    return (jnp.cos(angle_pair) * MSCALE)[None, :, None, :], (jnp.sin(angle_pair) * MSCALE)[None, :, None, :]


def rotate_half(values):
    half = values.shape[-1] // 2
    return jnp.concatenate([-values[..., half:], values[..., :half]], axis=-1)


def masked_scores(q_blk, k_blk, q_start, k_start, scale):
    scores = jnp.einsum('bqhd,bkhd->bhqk', q_blk, k_blk, preferred_element_type=jnp.float32) * scale
    q_pos = q_start + jnp.arange(q_blk.shape[1])[:, None]
    k_pos = k_start + jnp.arange(k_blk.shape[1])[None, :]
    return jnp.where(k_pos <= q_pos, scores, MASK_VALUE)


def fwd_block(stats, q_blk, k_blk, v_blk, q_start, k_start, scale):
    out_acc, row_max, row_sum = stats
    scores = masked_scores(q_blk, k_blk, q_start, k_start, scale)
    new_max = jnp.maximum(row_max, jnp.max(scores, axis=-1, keepdims=True))
    rescale = jnp.exp(row_max - new_max)
    attn_probs = jnp.exp(scores - new_max)
    row_sum = row_sum * rescale + jnp.sum(attn_probs, axis=-1, keepdims=True)
    pv_part = jnp.einsum('bhqk,bkhd->bqhd', attn_probs.astype(jnp.bfloat16), v_blk, preferred_element_type=jnp.float32)
    out_acc = out_acc * jnp.transpose(rescale, (0, 2, 1, 3)) + pv_part
    return out_acc, new_max, row_sum


def bwd_block(q_blk, k_blk, v_blk, d_attn, log_norm, delta, q_start, k_start, scale):
    attn_probs = jnp.exp(masked_scores(q_blk, k_blk, q_start, k_start, scale) - log_norm)
    dv_part = jnp.einsum('bhqk,bqhd->bkhd', attn_probs.astype(jnp.bfloat16), d_attn, preferred_element_type=jnp.float32)
    d_probs = jnp.einsum('bqhd,bkhd->bhqk', d_attn, v_blk, preferred_element_type=jnp.float32)
    d_scores = (attn_probs * (d_probs - delta) * scale).astype(jnp.bfloat16)
    dq_part = jnp.einsum('bhqk,bkhd->bqhd', d_scores, k_blk, preferred_element_type=jnp.float32)
    dk_part = jnp.einsum('bhqk,bqhd->bkhd', d_scores, q_blk, preferred_element_type=jnp.float32)
    return dq_part, dk_part, dv_part


def solution(mesh):
    cp_size = mesh.shape['cp']
    shift_perm = [(src_dev, (src_dev + 1) % cp_size) for src_dev in range(cp_size)]

    def device_fn(x_in, positions, long_factor, norm_gain, w_qkv, w_out, grad_y):
        batch, piece, hidden = x_in.shape
        head_dim = 2 * long_factor.shape[0]
        width = w_out.shape[0]
        heads = width // head_dim
        scale = 1.0 / math.sqrt(head_dim)
        my_index = lax.axis_index('cp')
        q_start = my_index * piece
        x_float = x_in.astype(jnp.float32)
        inv_rms = lax.rsqrt(jnp.mean(x_float * x_float, axis=-1, keepdims=True) + NORM_EPS)
        x_hat = x_float * inv_rms
        normed = (x_hat * norm_gain).astype(jnp.bfloat16)
        qkv_proj = jnp.einsum('bsd,de->bse', normed, w_qkv, preferred_element_type=jnp.float32)
        qkv_proj = qkv_proj.reshape(batch, piece, 3, heads, head_dim)
        cos_tab, sin_tab = rope_tables(positions, long_factor)
        q_rot = (qkv_proj[:, :, 0] * cos_tab + rotate_half(qkv_proj[:, :, 0]) * sin_tab).astype(jnp.bfloat16)
        k_rot = (qkv_proj[:, :, 1] * cos_tab + rotate_half(qkv_proj[:, :, 1]) * sin_tab).astype(jnp.bfloat16)
        v_val = qkv_proj[:, :, 2].astype(jnp.bfloat16)

        init_stats = (jnp.zeros((batch, piece, heads, head_dim), jnp.float32), jnp.full((batch, heads, piece, 1), MASK_VALUE, jnp.float32), jnp.zeros((batch, heads, piece, 1), jnp.float32))
        stats = fwd_block(init_stats, q_rot, k_rot, v_val, q_start, q_start, scale)

        def fwd_step(step_idx, state):
            stats, k_cur, v_cur = state
            k_cur = lax.ppermute(k_cur, 'cp', shift_perm)
            v_cur = lax.ppermute(v_cur, 'cp', shift_perm)
            k_start = (my_index - step_idx) * piece
            stats = lax.cond(step_idx <= my_index, lambda acc: fwd_block(acc, q_rot, k_cur, v_cur, q_start, k_start, scale), lambda acc: acc, stats)
            return stats, k_cur, v_cur

        stats, _, _ = lax.fori_loop(1, cp_size, fwd_step, (stats, k_rot, v_val))
        out_acc, row_max, row_sum = stats
        attn_out = (out_acc / jnp.transpose(row_sum, (0, 2, 1, 3))).astype(jnp.bfloat16)
        log_norm = row_max + jnp.log(row_sum)
        attn_flat = attn_out.reshape(batch, piece, width)
        y_out = (x_float + jnp.einsum('bsh,hd->bsd', attn_flat, w_out, preferred_element_type=jnp.float32)).astype(jnp.bfloat16)

        d_attn = jnp.einsum('bsd,hd->bsh', grad_y, w_out, preferred_element_type=jnp.float32).astype(jnp.bfloat16).reshape(batch, piece, heads, head_dim)
        g_wout = jnp.einsum('bsh,bsd->hd', attn_flat, grad_y, preferred_element_type=jnp.float32)
        delta = jnp.einsum('bqhd,bqhd->bhq', d_attn, attn_out, preferred_element_type=jnp.float32)[..., None]
        dq_acc, dk_own, dv_own = bwd_block(q_rot, k_rot, v_val, d_attn, log_norm, delta, q_start, q_start, scale)

        def bwd_step(step_idx, state):
            dq_acc, k_cur, v_cur, dk_cur, dv_cur = state
            k_cur = lax.ppermute(k_cur, 'cp', shift_perm)
            v_cur = lax.ppermute(v_cur, 'cp', shift_perm)
            dk_cur = lax.ppermute(dk_cur, 'cp', shift_perm)
            dv_cur = lax.ppermute(dv_cur, 'cp', shift_perm)
            k_start = (my_index - step_idx) * piece

            def add_block(sums):
                dq_sum, dk_sum, dv_sum = sums
                dq_part, dk_part, dv_part = bwd_block(q_rot, k_cur, v_cur, d_attn, log_norm, delta, q_start, k_start, scale)
                return dq_sum + dq_part, dk_sum + dk_part, dv_sum + dv_part

            dq_acc, dk_cur, dv_cur = lax.cond(step_idx <= my_index, add_block, lambda sums: sums, (dq_acc, dk_cur, dv_cur))
            return dq_acc, k_cur, v_cur, dk_cur, dv_cur

        dq_acc, _, _, dk_cur, dv_cur = lax.fori_loop(1, cp_size, bwd_step, (dq_acc, k_rot, v_val, dk_own, dv_own))
        dk_home = lax.ppermute(dk_cur, 'cp', shift_perm)
        dv_home = lax.ppermute(dv_cur, 'cp', shift_perm)

        dq_raw = dq_acc * cos_tab - rotate_half(dq_acc * sin_tab)
        dk_raw = dk_home * cos_tab - rotate_half(dk_home * sin_tab)
        d_qkv = jnp.stack([dq_raw.astype(jnp.bfloat16), dk_raw.astype(jnp.bfloat16), dv_home.astype(jnp.bfloat16)], axis=2).reshape(batch, piece, 3 * width)
        g_wqkv = jnp.einsum('bsd,bse->de', normed, d_qkv, preferred_element_type=jnp.float32)
        d_normed = jnp.einsum('bse,de->bsd', d_qkv, w_qkv, preferred_element_type=jnp.float32)
        g_gain = jnp.sum(d_normed * x_hat, axis=(0, 1))
        d_hat = d_normed * norm_gain
        dx_norm = inv_rms * (d_hat - x_hat * jnp.mean(d_hat * x_hat, axis=-1, keepdims=True))
        grad_x = (grad_y.astype(jnp.float32) + dx_norm).astype(jnp.bfloat16)
        g_gain, g_wqkv, g_wout = lax.psum((g_gain, g_wqkv, g_wout), 'cp')
        return y_out, grad_x, g_gain, g_wqkv, g_wout

    seq_spec = P('dp', 'cp', None)
    return jax.shard_map(device_fn, mesh=mesh, in_specs=(seq_spec, P(('dp', 'cp')), P(None), P(None), P(None, None), P(None, None), seq_spec), out_specs=(seq_spec, seq_spec, P('dp'), P('dp', None), P('dp', None)), check_vma=False)
```

profile of v0, /device:TPU:0, one launch (start us, length us, event | category | flops | bytes accessed | tf_op | source)
XLA Modules:
  0.0 3600.8 jit_solution(16977284657618973259)
XLA Ops:
  10.6 40.8 %fusion.31 = f32[3,384,6144]{1,2,0:T(8,128)} fusion(bf16[2048,6144]{1,0:T(8,128)(2,1)} %param.19, bf16[3,384,2048]{2,1,0:T(8,128)(2,1)} %param.15, f32[2048]{0:T(1024)} %param.18, f32[3,384]{1,0:T(4,128)S(1)} %add_rsqrt_fusion), kind=kOutput, calls=%fused_computation.45 | convolution fusion | flops 29000466432 | bytes 58208768 | tf_op jit(solution)/shard_map/bsd,de->bse/dot_general | solution.py:71
  110.3 25.0 fusion.22
  153.9 26.8 bitcast_add_fusion.5
  207.5 482.9 %while.42 = (s32[]{:T(128)}, f32[3,384,32,64]{1,3,2,0:T(8,128)}, f32[3,32,384,1]{2,1,0,3:T(8,128)S(1)}, f32[3,32,384,1]{2,1,0,3:T(8,128)S(1)}, bf16[3,384,32,64]...) while((s32[]{:T(128)}, f32[3,384,32,64]{1,3,2,0:T(8,128)}, ...), condition=%wide.region_8.9_spmd, body=%wide.region_3.8_spmd.sunk | while | flops 3784569600 | bytes 262478176 | solution.py:89
  211.4 51.1 %collective-permute-done = bf16[3,384,32,64]{1,3,2,0:T(8,128)(2,1)} collective-permute-done((bf16[3,384,32,64]{1,3,2,0:T(8,128)(2,1)}, bf16[3,384,32,64]{1,3,2,0:T(8,128)(2,1)}, u32[]{:S(2)}, u32[]{:S(2)}) %collective-permute-start) | collective-permute-done | bytes 4718624 | tf_op jit(solution)/shard_map/while/body/eval_jaxpr/ppermute | solution.py:83
  262.6 50.6 %collective-permute-done.1 = bf16[3,384,32,64]{1,3,2,0:T(8,128)(2,1)} collective-permute-done((bf16[3,384,32,64]{1,3,2,0:T(8,128)(2,1)}, bf16[3,384,32,64]{1,3,2,0:T(8,128)(2,1)}, u32[]{:S(2)}, u32[]{:S(2)}) %collective-permute-start.1) | collective-permute-done | bytes 4718624 | tf_op jit(solution)/shard_map/while/body/eval_jaxpr/ppermute | solution.py:84
  323.0 72.1 %collective-permute-start = (bf16[3,384,32,64]{1,3,2,0:T(8,128)(2,1)}, bf16[3,384,32,64]{1,3,2,0:T(8,128)(2,1)}, u32[]{:S(2)}, u32[]{:S(2)}) collective-permute-start(bf16[3,384,32,64]{1,3,2,0:T(8,128)(2,1)} %get-tuple-element.770), channel_id=1, source_target_pairs={{0,1},{1,2},{2,3},{3,0},{4,5},{5,6},{6,7},{7,4}} | collective-permute-start | bytes 14155784 | tf_op jit(solution)/shard_map/while/body/eval_jaxpr/ppermute | solution.py:83
  397.6 48.7 %collective-permute-done = bf16[3,384,32,64]{1,3,2,0:T(8,128)(2,1)} collective-permute-done((bf16[3,384,32,64]{1,3,2,0:T(8,128)(2,1)}, bf16[3,384,32,64]{1,3,2,0:T(8,128)(2,1)}, u32[]{:S(2)}, u32[]{:S(2)}) %collective-permute-start) | collective-permute-done | bytes 4718624 | tf_op jit(solution)/shard_map/while/body/eval_jaxpr/ppermute | solution.py:83
  446.2 50.6 %collective-permute-done.1 = bf16[3,384,32,64]{1,3,2,0:T(8,128)(2,1)} collective-permute-done((bf16[3,384,32,64]{1,3,2,0:T(8,128)(2,1)}, bf16[3,384,32,64]{1,3,2,0:T(8,128)(2,1)}, u32[]{:S(2)}, u32[]{:S(2)}) %collective-permute-start.1) | collective-permute-done | bytes 4718624 | tf_op jit(solution)/shard_map/while/body/eval_jaxpr/ppermute | solution.py:84
  509.1 74.7 %collective-permute-start.1 = (bf16[3,384,32,64]{1,3,2,0:T(8,128)(2,1)}, bf16[3,384,32,64]{1,3,2,0:T(8,128)(2,1)}, u32[]{:S(2)}, u32[]{:S(2)}) collective-permute-start(bf16[3,384,32,64]{1,3,2,0:T(8,128)(2,1)} %get-tuple-element.771), channel_id=1, source_target_pairs={{0,1},{1,2},{2,3},{3,0},{4,5},{5,6},{6,7},{7,4}} | collective-permute-start | bytes 14155784 | tf_op jit(solution)/shard_map/while/body/eval_jaxpr/ppermute | solution.py:84
  583.7 46.2 %collective-permute-done = bf16[3,384,32,64]{1,3,2,0:T(8,128)(2,1)} collective-permute-done((bf16[3,384,32,64]{1,3,2,0:T(8,128)(2,1)}, bf16[3,384,32,64]{1,3,2,0:T(8,128)(2,1)}, u32[]{:S(2)}, u32[]{:S(2)}) %collective-permute-start) | collective-permute-done | bytes 4718624 | tf_op jit(solution)/shard_map/while/body/eval_jaxpr/ppermute | solution.py:83
  629.9 50.6 %collective-permute-done.1 = bf16[3,384,32,64]{1,3,2,0:T(8,128)(2,1)} collective-permute-done((bf16[3,384,32,64]{1,3,2,0:T(8,128)(2,1)}, bf16[3,384,32,64]{1,3,2,0:T(8,128)(2,1)}, u32[]{:S(2)}, u32[]{:S(2)}) %collective-permute-start.1) | collective-permute-done | bytes 4718624 | tf_op jit(solution)/shard_map/while/body/eval_jaxpr/ppermute | solution.py:84
  691.0 26.0 fusion.69
  726.6 34.9 multiply_convert_fusion.1
  761.4 20.2 convolution_bitcast_fusion.2
  800.2 1313.3 %while.43 = (s32[]{:T(128)}, f32[3,384,32,64]{1,3,2,0:T(8,128)}, bf16[3,384,32,64]{1,3,2,0:T(8,128)(2,1)}, bf16[3,384,32,64]{1,3,2,0:T(8,128)(2,1)}, f32[3,384,3...) while((s32[]{:T(128)}, f32[3,384,32,64]{1,3,2,0:T(8,128)}, ...), condition=%wide.region_12.13_spmd, body=%wide.region_9.12_spmd.sunk | while | flops 9222636544 | bytes 515217888 | solution.py:117
  808.0 64.6 %collective-permute-start.4 = (bf16[3,384,32,64]{1,3,2,0:T(8,128)(2,1)}, bf16[3,384,32,64]{1,3,2,0:T(8,128)(2,1)}, u32[]{:S(2)}, u32[]{:S(2)}) collective-permute-start(bf16[3,384,32,64]{1,3,2,0:T(8,128)(2,1)} %get-tuple-element.801), channel_id=1, source_target_pairs={{0,1},{1,2},{2,3},{3,0},{4,5},{5,6},{6,7},{7,4}} | collective-permute-start | bytes 14155784 | tf_op jit(solution)/shard_map/while/body/eval_jaxpr/ppermute | solution.py:103
  872.6 253.5 %collective-permute-done.4 = bf16[3,384,32,64]{1,3,2,0:T(8,128)(2,1)} collective-permute-done((bf16[3,384,32,64]{1,3,2,0:T(8,128)(2,1)}, bf16[3,384,32,64]{1,3,2,0:T(8,128)(2,1)}, u32[]{:S(2)}, u32[]{:S(2)}) %collective-permute-start.4) | collective-permute-done | bytes 4718624 | tf_op jit(solution)/shard_map/while/body/eval_jaxpr/ppermute | solution.py:103
  1131.1 45.6 %collective-permute-done.5 = bf16[3,384,32,64]{1,3,2,0:T(8,128)(2,1)} collective-permute-done((bf16[3,384,32,64]{1,3,2,0:T(8,128)(2,1)}, bf16[3,384,32,64]{1,3,2,0:T(8,128)(2,1)}, u32[]{:S(2)}, u32[]{:S(2)}) %collective-permute-start.5) | collective-permute-done | bytes 4718624 | tf_op jit(solution)/shard_map/while/body/eval_jaxpr/ppermute | solution.py:104
  1198.8 66.4 %collective-permute-start.2 = (f32[3,384,32,64]{1,3,2,0:T(8,128)}, f32[3,384,32,64]{1,3,2,0:T(8,128)}, u32[]{:S(2)}, u32[]{:S(2)}) collective-permute-start(f32[3,384,32,64]{1,3,2,0:T(8,128)} %get-tuple-element.803), channel_id=1, source_target_pairs={{0,1},{1,2},{2,3},{3,0},{4,5},{5,6},{6,7},{7,4}} | collective-permute-start | bytes 28311560 | tf_op jit(solution)/shard_map/while/body/eval_jaxpr/ppermute | solution.py:105
  1267.7 62.1 %collective-permute-start.4 = (bf16[3,384,32,64]{1,3,2,0:T(8,128)(2,1)}, bf16[3,384,32,64]{1,3,2,0:T(8,128)(2,1)}, u32[]{:S(2)}, u32[]{:S(2)}) collective-permute-start(bf16[3,384,32,64]{1,3,2,0:T(8,128)(2,1)} %get-tuple-element.801), channel_id=1, source_target_pairs={{0,1},{1,2},{2,3},{3,0},{4,5},{5,6},{6,7},{7,4}} | collective-permute-start | bytes 14155784 | tf_op jit(solution)/shard_map/while/body/eval_jaxpr/ppermute | solution.py:103
  1329.8 253.5 %collective-permute-done.4 = bf16[3,384,32,64]{1,3,2,0:T(8,128)(2,1)} collective-permute-done((bf16[3,384,32,64]{1,3,2,0:T(8,128)(2,1)}, bf16[3,384,32,64]{1,3,2,0:T(8,128)(2,1)}, u32[]{:S(2)}, u32[]{:S(2)}) %collective-permute-start.4) | collective-permute-done | bytes 4718624 | tf_op jit(solution)/shard_map/while/body/eval_jaxpr/ppermute | solution.py:103
  1588.3 45.6 %collective-permute-done.5 = bf16[3,384,32,64]{1,3,2,0:T(8,128)(2,1)} collective-permute-done((bf16[3,384,32,64]{1,3,2,0:T(8,128)(2,1)}, bf16[3,384,32,64]{1,3,2,0:T(8,128)(2,1)}, u32[]{:S(2)}, u32[]{:S(2)}) %collective-permute-start.5) | collective-permute-done | bytes 4718624 | tf_op jit(solution)/shard_map/while/body/eval_jaxpr/ppermute | solution.py:104
  1656.1 71.4 %collective-permute-start.3 = (f32[3,384,32,64]{1,3,2,0:T(8,128)}, f32[3,384,32,64]{1,3,2,0:T(8,128)}, u32[]{:S(2)}, u32[]{:S(2)}) collective-permute-start(f32[3,384,32,64]{1,3,2,0:T(8,128)} %get-tuple-element.804), channel_id=1, source_target_pairs={{0,1},{1,2},{2,3},{3,0},{4,5},{5,6},{6,7},{7,4}} | collective-permute-start | bytes 28311560 | tf_op jit(solution)/shard_map/while/body/eval_jaxpr/ppermute | solution.py:106
  1727.5 59.6 %collective-permute-start.4 = (bf16[3,384,32,64]{1,3,2,0:T(8,128)(2,1)}, bf16[3,384,32,64]{1,3,2,0:T(8,128)(2,1)}, u32[]{:S(2)}, u32[]{:S(2)}) collective-permute-start(bf16[3,384,32,64]{1,3,2,0:T(8,128)(2,1)} %get-tuple-element.801), channel_id=1, source_target_pairs={{0,1},{1,2},{2,3},{3,0},{4,5},{5,6},{6,7},{7,4}} | collective-permute-start | bytes 14155784 | tf_op jit(solution)/shard_map/while/body/eval_jaxpr/ppermute | solution.py:103
  1787.1 253.5 %collective-permute-done.4 = bf16[3,384,32,64]{1,3,2,0:T(8,128)(2,1)} collective-permute-done((bf16[3,384,32,64]{1,3,2,0:T(8,128)(2,1)}, bf16[3,384,32,64]{1,3,2,0:T(8,128)(2,1)}, u32[]{:S(2)}, u32[]{:S(2)}) %collective-permute-start.4) | collective-permute-done | bytes 4718624 | tf_op jit(solution)/shard_map/while/body/eval_jaxpr/ppermute | solution.py:103
  2045.6 45.6 %collective-permute-done.5 = bf16[3,384,32,64]{1,3,2,0:T(8,128)(2,1)} collective-permute-done((bf16[3,384,32,64]{1,3,2,0:T(8,128)(2,1)}, bf16[3,384,32,64]{1,3,2,0:T(8,128)(2,1)}, u32[]{:S(2)}, u32[]{:S(2)}) %collective-permute-start.5) | collective-permute-done | bytes 4718624 | tf_op jit(solution)/shard_map/while/body/eval_jaxpr/ppermute | solution.py:104
  2136.0 210.4 %collective-permute-done.6 = f32[3,384,32,64]{1,3,2,0:T(8,128)} collective-permute-done((f32[3,384,32,64]{1,3,2,0:T(8,128)}, f32[3,384,32,64]{1,3,2,0:T(8,128)}, u32[]{:S(2)}, u32[]{:S(2)}) %collective-permute-start.6) | collective-permute-done | bytes 9437216 | tf_op jit(solution)/shard_map/ppermute | solution.py:118
  2412.3 40.7 %convolution_bitcast_fusion = f32[2048,6144]{1,0:T(8,128)} fusion(bf16[3,384,6144]{1,2,0:T(8,128)(2,1)S(1)} %bitcast.144, bf16[3,384,2048]{2,1,0:T(8,128)(2,1)S(1)} %bitcast.143, f32[2048]{0:T(1024)S(1)} %copy-done.14, f32[3,384]{1,0:T(4,128)S(1)} %copy-done.13), kind=kOutput, calls=%fused_computation.42 | convolution fusion | flops 29000466432 | bytes 69218816 | tf_op jit(solution)/shard_map/bsd,bse->de/dot_general | solution.py:124
  2469.0 41.6 %fusion.43 = (f32[2048]{0:T(1024)S(1)}, f32[3,384]{1,0:T(4,128)S(1)}, f32[3,384,2048]{2,1,0:T(8,128)}) fusion(bf16[3,384,2048]{2,1,0:T(8,128)(2,1)} %param.15, f32[3,384]{1,0:T(4,128)S(1)} %copy-done.13, f32[2048]{0:T(1024)S(1)} %copy-done.14, bf16[3,384,6144]{1,2,0:T(8,128)(2,1)} %bitcast.145, bf16[2048,6144]{1,0:T(8,128)(2,1)} %param.19), kind=kOutput, calls=%fused_computation.61 | convolution fusion | flops 29007540224 | bytes 53502976 | tf_op jit(solution)/shard_map/bse,de->bsd/dot_general | solution.py:125
  2527.9 1019.3 %all-reduce.3.cloned.1.call-done = (f32[2048,6144]{1,0:T(8,128)}, f32[2048,2048]{1,0:T(8,128)}) async-done(((f32[2048,6144]{1,0:T(8,128)}, f32[2048,2048]{1,0:T(8,128)}), (f32[2048,6144]{1,0:T(8,128)}, f32[2048,2048]{1,0:T(8,128)})) %all-reduce.3.cloned.1.call-update) | async-done | bytes 67108880 | tf_op jit(solution)/shard_map/psum | solution.py:130
  3547.2 34.5 copy.127
  (140 shorter events, 399.0 us)
Async XLA Ops:
  7.2 3540.0 %all-reduce.3.cloned.1.call-start = ((), (), s32[]{:S(2)}) async-start(), calls=%async_computation | async-start | bytes 134217728 | tf_op jit(solution)/shard_map/psum | solution.py:130
  10.6 40.8 %copy-start.12 = (f32[3,384]{1,0:T(4,128)}, f32[3,384]{1,0:T(4,128)S(1)}, u32[]{:S(2)}) copy-start(f32[3,384]{1,0:T(4,128)S(1)} %add_rsqrt_fusion) | copy-start | bytes 13828
  77.5 76.4 %copy-start.4 = (pred[384,384]{0,1:T(8,128)(4,1)}, pred[384,384]{0,1:T(8,128)(4,1)S(1)}, u32[]{:S(2)}) copy-start(pred[384,384]{0,1:T(8,128)(4,1)S(1)} %broadcast_compare_fusion.2) | copy-start | bytes 442372
  77.5 15.4 slice-start.5
  207.5 483.5 %copy-start.5 = (pred[384,384]{0,1:T(8,128)(4,1)S(1)}, pred[384,384]{0,1:T(8,128)(4,1)}, u32[]{:S(2)}) copy-start(pred[384,384]{0,1:T(8,128)(4,1)} %copy-done.4) | copy-start | bytes 442372
  208.0 54.6 %collective-permute-start = (bf16[3,384,32,64]{1,3,2,0:T(8,128)(2,1)}, bf16[3,384,32,64]{1,3,2,0:T(8,128)(2,1)}, u32[]{:S(2)}, u32[]{:S(2)}) collective-permute-start(bf16[3,384,32,64]{1,3,2,0:T(8,128)(2,1)} %get-tuple-element.770), channel_id=1, source_target_pairs={{0,1},{1,2},{2,3},{3,0},{4,5},{5,6},{6,7},{7,4}} | collective-permute-start | bytes 14155784 | tf_op jit(solution)/shard_map/while/body/eval_jaxpr/ppermute | solution.py:83
  208.8 104.3 %collective-permute-start.1 = (bf16[3,384,32,64]{1,3,2,0:T(8,128)(2,1)}, bf16[3,384,32,64]{1,3,2,0:T(8,128)(2,1)}, u32[]{:S(2)}, u32[]{:S(2)}) collective-permute-start(bf16[3,384,32,64]{1,3,2,0:T(8,128)(2,1)} %get-tuple-element.771), channel_id=1, source_target_pairs={{0,1},{1,2},{2,3},{3,0},{4,5},{5,6},{6,7},{7,4}} | collective-permute-start | bytes 14155784 | tf_op jit(solution)/shard_map/while/body/eval_jaxpr/ppermute | solution.py:84
  323.0 123.2 %collective-permute-start = (bf16[3,384,32,64]{1,3,2,0:T(8,128)(2,1)}, bf16[3,384,32,64]{1,3,2,0:T(8,128)(2,1)}, u32[]{:S(2)}, u32[]{:S(2)}) collective-permute-start(bf16[3,384,32,64]{1,3,2,0:T(8,128)(2,1)} %get-tuple-element.770), channel_id=1, source_target_pairs={{0,1},{1,2},{2,3},{3,0},{4,5},{5,6},{6,7},{7,4}} | collective-permute-start | bytes 14155784 | tf_op jit(solution)/shard_map/while/body/eval_jaxpr/ppermute | solution.py:83
  395.1 101.7 %collective-permute-start.1 = (bf16[3,384,32,64]{1,3,2,0:T(8,128)(2,1)}, bf16[3,384,32,64]{1,3,2,0:T(8,128)(2,1)}, u32[]{:S(2)}, u32[]{:S(2)}) collective-permute-start(bf16[3,384,32,64]{1,3,2,0:T(8,128)(2,1)} %get-tuple-element.771), channel_id=1, source_target_pairs={{0,1},{1,2},{2,3},{3,0},{4,5},{5,6},{6,7},{7,4}} | collective-permute-start | bytes 14155784 | tf_op jit(solution)/shard_map/while/body/eval_jaxpr/ppermute | solution.py:84
  506.7 123.2 %collective-permute-start = (bf16[3,384,32,64]{1,3,2,0:T(8,128)(2,1)}, bf16[3,384,32,64]{1,3,2,0:T(8,128)(2,1)}, u32[]{:S(2)}, u32[]{:S(2)}) collective-permute-start(bf16[3,384,32,64]{1,3,2,0:T(8,128)(2,1)} %get-tuple-element.770), channel_id=1, source_target_pairs={{0,1},{1,2},{2,3},{3,0},{4,5},{5,6},{6,7},{7,4}} | collective-permute-start | bytes 14155784 | tf_op jit(solution)/shard_map/while/body/eval_jaxpr/ppermute | solution.py:83
  509.1 171.4 %collective-permute-start.1 = (bf16[3,384,32,64]{1,3,2,0:T(8,128)(2,1)}, bf16[3,384,32,64]{1,3,2,0:T(8,128)(2,1)}, u32[]{:S(2)}, u32[]{:S(2)}) collective-permute-start(bf16[3,384,32,64]{1,3,2,0:T(8,128)(2,1)} %get-tuple-element.771), channel_id=1, source_target_pairs={{0,1},{1,2},{2,3},{3,0},{4,5},{5,6},{6,7},{7,4}} | collective-permute-start | bytes 14155784 | tf_op jit(solution)/shard_map/while/body/eval_jaxpr/ppermute | solution.py:84
  691.0 26.0 copy-start
  781.6 18.6 copy-start.11
  800.6 381.0 %collective-permute-start.2 = (f32[3,384,32,64]{1,3,2,0:T(8,128)}, f32[3,384,32,64]{1,3,2,0:T(8,128)}, u32[]{:S(2)}, u32[]{:S(2)}) collective-permute-start(f32[3,384,32,64]{1,3,2,0:T(8,128)} %get-tuple-element.803), channel_id=1, source_target_pairs={{0,1},{1,2},{2,3},{3,0},{4,5},{5,6},{6,7},{7,4}} | collective-permute-start | bytes 28311560 | tf_op jit(solution)/shard_map/while/body/eval_jaxpr/ppermute | solution.py:105
  805.5 376.1 %collective-permute-start.3 = (f32[3,384,32,64]{1,3,2,0:T(8,128)}, f32[3,384,32,64]{1,3,2,0:T(8,128)}, u32[]{:S(2)}, u32[]{:S(2)}) collective-permute-start(f32[3,384,32,64]{1,3,2,0:T(8,128)} %get-tuple-element.804), channel_id=1, source_target_pairs={{0,1},{1,2},{2,3},{3,0},{4,5},{5,6},{6,7},{7,4}} | collective-permute-start | bytes 28311560 | tf_op jit(solution)/shard_map/while/body/eval_jaxpr/ppermute | solution.py:106
  808.0 318.1 %collective-permute-start.4 = (bf16[3,384,32,64]{1,3,2,0:T(8,128)(2,1)}, bf16[3,384,32,64]{1,3,2,0:T(8,128)(2,1)}, u32[]{:S(2)}, u32[]{:S(2)}) collective-permute-start(bf16[3,384,32,64]{1,3,2,0:T(8,128)(2,1)} %get-tuple-element.801), channel_id=1, source_target_pairs={{0,1},{1,2},{2,3},{3,0},{4,5},{5,6},{6,7},{7,4}} | collective-permute-start | bytes 14155784 | tf_op jit(solution)/shard_map/while/body/eval_jaxpr/ppermute | solution.py:103
  872.5 304.1 %collective-permute-start.5 = (bf16[3,384,32,64]{1,3,2,0:T(8,128)(2,1)}, bf16[3,384,32,64]{1,3,2,0:T(8,128)(2,1)}, u32[]{:S(2)}, u32[]{:S(2)}) collective-permute-start(bf16[3,384,32,64]{1,3,2,0:T(8,128)(2,1)} %get-tuple-element.802), channel_id=1, source_target_pairs={{0,1},{1,2},{2,3},{3,0},{4,5},{5,6},{6,7},{7,4}} | collective-permute-start | bytes 14155784 | tf_op jit(solution)/shard_map/while/body/eval_jaxpr/ppermute | solution.py:104
  1198.8 440.0 %collective-permute-start.2 = (f32[3,384,32,64]{1,3,2,0:T(8,128)}, f32[3,384,32,64]{1,3,2,0:T(8,128)}, u32[]{:S(2)}, u32[]{:S(2)}) collective-permute-start(f32[3,384,32,64]{1,3,2,0:T(8,128)} %get-tuple-element.803), channel_id=1, source_target_pairs={{0,1},{1,2},{2,3},{3,0},{4,5},{5,6},{6,7},{7,4}} | collective-permute-start | bytes 28311560 | tf_op jit(solution)/shard_map/while/body/eval_jaxpr/ppermute | solution.py:105
  1265.2 373.6 %collective-permute-start.3 = (f32[3,384,32,64]{1,3,2,0:T(8,128)}, f32[3,384,32,64]{1,3,2,0:T(8,128)}, u32[]{:S(2)}, u32[]{:S(2)}) collective-permute-start(f32[3,384,32,64]{1,3,2,0:T(8,128)} %get-tuple-element.804), channel_id=1, source_target_pairs={{0,1},{1,2},{2,3},{3,0},{4,5},{5,6},{6,7},{7,4}} | collective-permute-start | bytes 28311560 | tf_op jit(solution)/shard_map/while/body/eval_jaxpr/ppermute | solution.py:106
  1267.7 315.6 %collective-permute-start.4 = (bf16[3,384,32,64]{1,3,2,0:T(8,128)(2,1)}, bf16[3,384,32,64]{1,3,2,0:T(8,128)(2,1)}, u32[]{:S(2)}, u32[]{:S(2)}) collective-permute-start(bf16[3,384,32,64]{1,3,2,0:T(8,128)(2,1)} %get-tuple-element.801), channel_id=1, source_target_pairs={{0,1},{1,2},{2,3},{3,0},{4,5},{5,6},{6,7},{7,4}} | collective-permute-start | bytes 14155784 | tf_op jit(solution)/shard_map/while/body/eval_jaxpr/ppermute | solution.py:103
  1329.8 304.1 %collective-permute-start.5 = (bf16[3,384,32,64]{1,3,2,0:T(8,128)(2,1)}, bf16[3,384,32,64]{1,3,2,0:T(8,128)(2,1)}, u32[]{:S(2)}, u32[]{:S(2)}) collective-permute-start(bf16[3,384,32,64]{1,3,2,0:T(8,128)(2,1)} %get-tuple-element.802), channel_id=1, source_target_pairs={{0,1},{1,2},{2,3},{3,0},{4,5},{5,6},{6,7},{7,4}} | collective-permute-start | bytes 14155784 | tf_op jit(solution)/shard_map/while/body/eval_jaxpr/ppermute | solution.py:104
  1656.1 440.0 %collective-permute-start.2 = (f32[3,384,32,64]{1,3,2,0:T(8,128)}, f32[3,384,32,64]{1,3,2,0:T(8,128)}, u32[]{:S(2)}, u32[]{:S(2)}) collective-permute-start(f32[3,384,32,64]{1,3,2,0:T(8,128)} %get-tuple-element.803), channel_id=1, source_target_pairs={{0,1},{1,2},{2,3},{3,0},{4,5},{5,6},{6,7},{7,4}} | collective-permute-start | bytes 28311560 | tf_op jit(solution)/shard_map/while/body/eval_jaxpr/ppermute | solution.py:105
  1656.1 440.0 %collective-permute-start.3 = (f32[3,384,32,64]{1,3,2,0:T(8,128)}, f32[3,384,32,64]{1,3,2,0:T(8,128)}, u32[]{:S(2)}, u32[]{:S(2)}) collective-permute-start(f32[3,384,32,64]{1,3,2,0:T(8,128)} %get-tuple-element.804), channel_id=1, source_target_pairs={{0,1},{1,2},{2,3},{3,0},{4,5},{5,6},{6,7},{7,4}} | collective-permute-start | bytes 28311560 | tf_op jit(solution)/shard_map/while/body/eval_jaxpr/ppermute | solution.py:106
  1727.5 313.1 %collective-permute-start.4 = (bf16[3,384,32,64]{1,3,2,0:T(8,128)(2,1)}, bf16[3,384,32,64]{1,3,2,0:T(8,128)(2,1)}, u32[]{:S(2)}, u32[]{:S(2)}) collective-permute-start(bf16[3,384,32,64]{1,3,2,0:T(8,128)(2,1)} %get-tuple-element.801), channel_id=1, source_target_pairs={{0,1},{1,2},{2,3},{3,0},{4,5},{5,6},{6,7},{7,4}} | collective-permute-start | bytes 14155784 | tf_op jit(solution)/shard_map/while/body/eval_jaxpr/ppermute | solution.py:103
  1787.1 304.1 %collective-permute-start.5 = (bf16[3,384,32,64]{1,3,2,0:T(8,128)(2,1)}, bf16[3,384,32,64]{1,3,2,0:T(8,128)(2,1)}, u32[]{:S(2)}, u32[]{:S(2)}) collective-permute-start(bf16[3,384,32,64]{1,3,2,0:T(8,128)(2,1)} %get-tuple-element.802), channel_id=1, source_target_pairs={{0,1},{1,2},{2,3},{3,0},{4,5},{5,6},{6,7},{7,4}} | collective-permute-start | bytes 14155784 | tf_op jit(solution)/shard_map/while/body/eval_jaxpr/ppermute | solution.py:104
  2113.5 232.9 %collective-permute-start.6 = (f32[3,384,32,64]{1,3,2,0:T(8,128)}, f32[3,384,32,64]{1,3,2,0:T(8,128)}, u32[]{:S(2)}, u32[]{:S(2)}) collective-permute-start(f32[3,384,32,64]{1,3,2,0:T(8,128)} %get-tuple-element.507), channel_id=1, source_target_pairs={{0,1},{1,2},{2,3},{3,0},{4,5},{5,6},{6,7},{7,4}} | collective-permute-start | bytes 28311560 | tf_op jit(solution)/shard_map/ppermute | solution.py:118
  2113.5 232.8 %slice-start = ((s8[9437184]{0:T(1024)(128)(4,1)}), s8[4194304]{0:T(1024)(128)(4,1)S(1)}, s32[]{:S(2)}) async-start(s8[9437184]{0:T(1024)(128)(4,1)} %bitcast.123), calls=%async_computation.1 | async-start | bytes 8388608
  2120.5 276.5 %collective-permute-start.7 = (bf16[3,384,32,64]{1,3,2,0:T(8,128)(2,1)}, bf16[3,384,32,64]{1,3,2,0:T(8,128)(2,1)}, u32[]{:S(2)}, u32[]{:S(2)}) collective-permute-start(bf16[3,384,32,64]{1,3,2,0:T(8,128)(2,1)} %convert.22), channel_id=1, source_target_pairs={{0,1},{1,2},{2,3},{3,0},{4,5},{5,6},{6,7},{7,4}} | collective-permute-start | bytes 14155784 | tf_op jit(solution)/shard_map/ppermute | solution.py:119
  2120.5 225.9 %slice-start.1 = ((s8[9437184]{0:T(1024)(128)(4,1)}), s8[4194304]{0:T(1024)(128)(4,1)S(1)}, s32[]{:S(2)}) async-start(s8[9437184]{0:T(1024)(128)(4,1)} %bitcast.123), calls=%async_computation.2 | async-start | bytes 8388608
  2120.5 225.9 %slice-start.2 = ((s8[9437184]{0:T(1024)(128)(4,1)}), s8[1048576]{0:T(1024)(128)(4,1)S(1)}, s32[]{:S(2)}) async-start(s8[9437184]{0:T(1024)(128)(4,1)} %bitcast.123), calls=%async_computation.3 | async-start | bytes 2097152
  2120.5 225.9 %copy-start.10 = (f32[384,64]{0,1:T(8,128)S(1)}, f32[384,64]{0,1:T(8,128)}, u32[]{:S(2)}) copy-start(f32[384,64]{0,1:T(8,128)} %copy-done.9) | copy-start | bytes 294916
  2396.9 15.3 slice-start.6
  (16 other events, 140.2 us)
Sparse Core Ops, SparseCore 0:
  2453.2 1093.9 all-reduce.2
where the time goes:
time: 3610 us; the launch traced here: 3600 us
  waiting for transfers between devices  2430 us (67%)
  starting transfers between devices  489 us (14%)
  matrix products  321 us (9%)
  local copies, waits for them, and re-layouts  210 us (6%)
  other arithmetic  124 us (3%)
    psum x1, waiting for transfers between devices, device_fn(): g_gain, g_wqkv, g_wout = lax.psum((g_gain, g_wqkv, g_wout), 'cp')  1020 us
    ppermute x3, waiting for transfers between devices, bwd_step(): k_cur = lax.ppermute(k_cur, 'cp', shift_perm)  761 us
    ppermute x1, waiting for transfers between devices, device_fn(): dk_home = lax.ppermute(dk_cur, 'cp', shift_perm)  210 us
    ppermute x3, starting transfers between devices, bwd_step(): k_cur = lax.ppermute(k_cur, 'cp', shift_perm)  186 us
    ppermute x3, waiting for transfers between devices, fwd_step(): v_cur = lax.ppermute(v_cur, 'cp', shift_perm)  152 us
    ppermute x3, waiting for transfers between devices, fwd_step(): k_cur = lax.ppermute(k_cur, 'cp', shift_perm)  146 us
    ppermute x3, waiting for transfers between devices, bwd_step(): v_cur = lax.ppermute(v_cur, 'cp', shift_perm)  137 us
    while x18, local copies, waits for them, and re-layouts  111 us
  transfers between devices with their start and end apart: 21, of which 15 were waited for; matrix products, arithmetic and copies ran while one was open for 4% of the time, Pallas kernels for 0%

commit v1 on v0

v1 whole, which is shorter than its diff:
```python
import math
import functools
import jax
import jax.numpy as jnp
from jax import lax
from jax.experimental import pallas as pl
from jax.experimental.pallas import tpu as pltpu
from jax.sharding import PartitionSpec as P

NORM_EPS = 1e-5
MSCALE = math.sqrt(1.0 + math.log(32.0) / math.log(4096.0))
MASK_VALUE = -1e30
VMEM_LIMIT = 60 * 1024 * 1024
NT = (((1,), (1,)), ((), ()))
NN = (((1,), (0,)), ((), ()))
TN = (((0,), (0,)), ((), ()))


def dot(a, b, dims):
    return lax.dot_general(a, b, dims, preferred_element_type=jnp.float32)


def params(semantics):
    return pltpu.CompilerParams(dimension_semantics=semantics, vmem_limit_bytes=VMEM_LIMIT)


def cost(flops, nbytes):
    return pl.CostEstimate(flops=int(flops), bytes_accessed=int(nbytes), transcendentals=0)


def proj_kernel(w_ref, xa_ref, xb_ref, da_ref, db_ref, gain_ref, cos_ref, sin_ref, out_ref, r_ref, dy_ref, *, head_dim, row_blocks, scale):
    step = pl.program_id(1)
    piece = xa_ref.shape[1]
    half = head_dim // 2

    @pl.when(step == 0)
    def _():
        for idx, ref in enumerate((xa_ref, xb_ref)):
            x = ref[0].astype(jnp.float32)
            inv = lax.rsqrt(jnp.mean(x * x, axis=-1, keepdims=True) + NORM_EPS)
            r_ref[0, idx * piece:(idx + 1) * piece, :] = (x * inv * gain_ref[...]).astype(jnp.bfloat16)
        dy_ref[0, :piece, :] = da_ref[0]
        dy_ref[0, piece:, :] = db_ref[0]

    @pl.when(step < 2 * row_blocks)
    def _():
        acc = dot(w_ref[...], r_ref[0], NT)
        factor = jnp.where(step < row_blocks, scale, 1.0).astype(jnp.float32)
        cos = cos_ref[0] * factor
        sin = sin_ref[0] * factor
        for head in range(w_ref.shape[0] // head_dim):
            lo = head * head_dim
            first = acc[lo:lo + half]
            second = acc[lo + half:lo + head_dim]
            out_ref[0, lo:lo + half, :] = (first * cos - second * sin).astype(jnp.bfloat16)
            out_ref[0, lo + half:lo + head_dim, :] = (second * cos + first * sin).astype(jnp.bfloat16)

    @pl.when((step >= 2 * row_blocks) & (step < 3 * row_blocks))
    def _():
        out_ref[0] = dot(w_ref[...], r_ref[0], NT).astype(jnp.bfloat16)

    @pl.when(step >= 3 * row_blocks)
    def _():
        out_ref[0] = dot(w_ref[...], dy_ref[0], NT).astype(jnp.bfloat16)


def project(w_cat, x_own, x_other, dy_own, dy_other, gain, cos, sin, head_dim):
    seqs, piece, hidden = x_own.shape
    rows = w_cat.shape[0]
    block = 512
    steps = rows // block
    pair = 2 * piece
    tok_spec = pl.BlockSpec((1, piece, hidden), lambda s, j: (s, 0, 0))
    tab_spec = pl.BlockSpec((1, head_dim // 2, pair), lambda s, j: (0, 0, 0))
    cat_spec = pl.BlockSpec((1, pair, hidden), lambda s, j: (s, 0, 0))
    return pl.pallas_call(
        functools.partial(proj_kernel, head_dim=head_dim, row_blocks=steps // 4, scale=1.0 / math.sqrt(head_dim)),
        grid=(seqs, steps),
        in_specs=[pl.BlockSpec((block, hidden), lambda s, j: (j, 0)), tok_spec, tok_spec, tok_spec, tok_spec,
                  pl.BlockSpec((1, hidden), lambda s, j: (0, 0)), tab_spec, tab_spec],
        out_specs=[pl.BlockSpec((1, block, pair), lambda s, j: (s, j, 0)), cat_spec, cat_spec],
        out_shape=[jax.ShapeDtypeStruct((seqs, rows, pair), jnp.bfloat16), jax.ShapeDtypeStruct((seqs, pair, hidden), jnp.bfloat16),
                   jax.ShapeDtypeStruct((seqs, pair, hidden), jnp.bfloat16)],
        compiler_params=params(('arbitrary', 'arbitrary')),
        cost_estimate=cost(2 * seqs * pair * hidden * rows, 2 * (rows * hidden + 5 * seqs * pair * hidden)),
        name='project',
    )(w_cat, x_own, x_other, dy_own, dy_other, gain, cos, sin)


def attn_kernel(*refs, head_dim, piece, tile):
    loc_refs, rem_refs = refs[0:4], refs[4:8]
    cos_ref, sin_ref, grads_ref, out_ref, feat, tok, s_scr, p_scr, dk_scr, dv_scr, dq_scr, o_scr = refs[8:]
    half = head_dim // 2
    n_tiles = 4 * piece // tile
    me = lax.axis_index('cp')
    mate = me + 1 - 2 * lax.rem(me, 2)
    places = [me, mate, lax.rem(me + 2, 4), lax.rem(mate + 2, 4)]
    spans = [pl.ds(pl.multiple_of(place * piece, 128), piece) for place in places]
    for idx in range(4):
        for rel in range(4):
            source = (loc_refs, rem_refs)[rel // 2][idx]
            lo = (rel % 2) * piece
            feat[idx, :, spans[rel]] = source[0, :, lo:lo + piece]
    for slot, idx in enumerate((1, 2)):
        tok[slot] = jnp.transpose(feat[idx])
    dk_scr[...] = jnp.zeros_like(dk_scr)
    dv_scr[...] = jnp.zeros_like(dv_scr)
    k_pos = lax.broadcasted_iota(jnp.int32, (tile, tile), 0)
    q_pos = lax.broadcasted_iota(jnp.int32, (tile, tile), 1)
    causal = k_pos <= q_pos

    for qi in range(n_tiles):
        qs = slice(qi * tile, (qi + 1) * tile)
        q_t = feat[0, :, qs]
        do_t = feat[3, :, qs]
        row_max = None
        for ki in range(qi + 1):
            ks = slice(ki * tile, (ki + 1) * tile)
            s = dot(tok[0, ks, :], q_t, NN)
            if ki == qi:
                s = jnp.where(causal, s, MASK_VALUE)
            s_scr[ks, :] = s
            cur = jnp.max(s, axis=0, keepdims=True)
            row_max = cur if row_max is None else jnp.maximum(row_max, cur)
        row_sum = jnp.zeros((1, tile), jnp.float32)
        for ki in range(qi + 1):
            ks = slice(ki * tile, (ki + 1) * tile)
            p = jnp.exp(s_scr[ks, :] - row_max)
            s_scr[ks, :] = p
            row_sum = row_sum + jnp.sum(p, axis=0, keepdims=True)
        inv = 1.0 / row_sum
        o_t = jnp.zeros((head_dim, tile), jnp.float32)
        for ki in range(qi + 1):
            ks = slice(ki * tile, (ki + 1) * tile)
            p = s_scr[ks, :] * inv
            s_scr[ks, :] = p
            p_low = p.astype(jnp.bfloat16)
            p_scr[ks, :] = p_low
            o_t = o_t + dot(feat[2, :, ks], p_low, NN)
        o_scr[:, qs] = o_t.astype(jnp.bfloat16)
        delta = jnp.sum(do_t.astype(jnp.float32) * o_t, axis=0, keepdims=True)
        dq_t = jnp.zeros((head_dim, tile), jnp.float32)
        for ki in range(qi + 1):
            ks = slice(ki * tile, (ki + 1) * tile)
            dp = dot(tok[1, ks, :], do_t, NN)
            ds = (s_scr[ks, :] * (dp - delta)).astype(jnp.bfloat16)
            dq_t = dq_t + dot(feat[1, :, ks], ds, NN)
            dk_scr[:, ks] += dot(q_t, ds, NT)
            dv_scr[:, ks] += dot(do_t, p_scr[ks, :], NT)
        dq_scr[:, qs] = dq_t * (1.0 / math.sqrt(head_dim))

    cos, sin = cos_ref[...], sin_ref[...]
    for slot, scr in enumerate((dq_scr, dk_scr)):
        first, second = scr[:half, :], scr[half:, :]
        scr[:half, :] = first * cos + second * sin
        scr[half:, :] = second * cos - first * sin
    for rel in range(4):
        side, lo = rel // 2, (rel % 2) * piece
        for slot, scr in enumerate((dq_scr, dk_scr, dv_scr)):
            grads_ref[side, slot, :, lo:lo + piece] = scr[:, spans[rel]].astype(jnp.bfloat16)
        out_ref[side, :, lo:lo + piece] = o_scr[:, spans[rel]]


def attention(seq, loc, rem, cos, sin, head_dim, tile=256):
    rows, pair = loc.shape[1:]
    part = rows // 4
    heads = part // head_dim
    length = 2 * pair
    half = head_dim // 2

    def head_spec(which, at):
        return pl.BlockSpec((1, head_dim, pair), lambda h: (at, which * heads + h, 0))

    tab_spec = pl.BlockSpec((half, length), lambda h: (0, 0))
    elems = heads * length * length // 2
    return pl.pallas_call(
        functools.partial(attn_kernel, head_dim=head_dim, piece=pair // 2, tile=tile),
        grid=(heads,),
        in_specs=[head_spec(w, seq) for w in range(4)] + [head_spec(w, 0) for w in range(4)] + [tab_spec, tab_spec],
        out_specs=[pl.BlockSpec((2, 3, head_dim, pair), lambda h: (0, 0, h, 0)), pl.BlockSpec((2, head_dim, pair), lambda h: (0, h, 0))],
        out_shape=[jax.ShapeDtypeStruct((2, 3, part, pair), jnp.bfloat16), jax.ShapeDtypeStruct((2, part, pair), jnp.bfloat16)],
        scratch_shapes=[pltpu.VMEM((4, head_dim, length), jnp.bfloat16), pltpu.VMEM((2, length, head_dim), jnp.bfloat16),
                        pltpu.VMEM((length, tile), jnp.float32), pltpu.VMEM((length, tile), jnp.bfloat16),
                        pltpu.VMEM((head_dim, length), jnp.float32), pltpu.VMEM((head_dim, length), jnp.float32),
                        pltpu.VMEM((head_dim, length), jnp.float32), pltpu.VMEM((head_dim, length), jnp.bfloat16)],
        compiler_params=params(('arbitrary',)),
        cost_estimate=cost(elems * 2 * 256 * 6, 2 * 8 * length * part),
        name='attention',
    )(*([loc] * 4), *([rem] * 4), cos, sin)


def grad_qkv_kernel(*refs):
    out_ref = refs[-1]
    acc = None
    for r_ref, g_refs in ((refs[0], refs[4:7]), ) :
        for seq in range(3):
            term = dot(r_ref[seq], g_refs[seq][0, 0], (((0,), (1,)), ((), ())))
            acc = term if acc is None else acc + term
    for seq in range(3):
        acc = acc + dot(refs[1 + seq][0], refs[4 + seq][1, 0], (((0,), (1,)), ((), ())))
    out_ref[...] = acc


def grad_qkv(r_loc, r_rems, grads, which):
    hidden = r_loc.shape[-1]
    pair = r_loc.shape[1]
    part = grads[0].shape[2]
    bm, bn = 512, 512
    return pl.pallas_call(
        grad_qkv_kernel,
        grid=(part // bn, hidden // bm),
        in_specs=[pl.BlockSpec((3, pair, bm), lambda n, m: (0, 0, m))] + [pl.BlockSpec((1, pair, bm), lambda n, m: (0, 0, m))] * 3
        + [pl.BlockSpec((2, 1, bn, pair), lambda n, m: (0, which, n, 0))] * 3,
        out_specs=pl.BlockSpec((bm, bn), lambda n, m: (m, n)),
        out_shape=jax.ShapeDtypeStruct((hidden, part), jnp.float32),
        compiler_params=params(('arbitrary', 'arbitrary')),
        cost_estimate=cost(2 * 6 * pair * hidden * part, 4 * hidden * part + 12 * pair * (hidden + part)),
        name='grad_qkv',
    )(r_loc, *r_rems, *grads)


def grad_out_kernel(*refs):
    out_ref = refs[-1]
    acc = None
    for seq in range(3):
        term = dot(refs[4 + seq][0], refs[0][seq], NN)
        acc = term if acc is None else acc + term
    for seq in range(3):
        acc = acc + dot(refs[4 + seq][1], refs[1 + seq][0], NN)
    out_ref[...] = acc


def grad_out(dy_loc, dy_rems, outs):
    hidden = dy_loc.shape[-1]
    pair = dy_loc.shape[1]
    part = outs[0].shape[1]
    bm, bn = 512, 512
    return pl.pallas_call(
        grad_out_kernel,
        grid=(hidden // bn, part // bm),
        in_specs=[pl.BlockSpec((3, pair, bn), lambda n, m: (0, 0, n))] + [pl.BlockSpec((1, pair, bn), lambda n, m: (0, 0, n))] * 3
        + [pl.BlockSpec((2, bm, pair), lambda n, m: (0, m, 0))] * 3,
        out_specs=pl.BlockSpec((bm, bn), lambda n, m: (m, n)),
        out_shape=jax.ShapeDtypeStruct((part, hidden), jnp.float32),
        compiler_params=params(('arbitrary', 'arbitrary')),
        cost_estimate=cost(2 * 6 * pair * hidden * part, 4 * hidden * part + 12 * pair * (hidden + part)),
        name='grad_out',
    )(dy_loc, *dy_rems, *outs)


def solution(mesh):
    mate_perm = [(i, i ^ 1) for i in range(4)]
    cross_perm = [(i, i ^ 2) for i in range(4)]

    def device_fn(x_in, positions, long_factor, norm_gain, w_qkv, w_out, grad_y):
        seqs, piece, hidden = x_in.shape
        half = long_factor.shape[0]
        head_dim = 2 * half
        width = w_out.shape[0]
        part = width // 2
        me = lax.axis_index('cp')
        core = lax.rem(me, 2)
        mate = me + 1 - 2 * core

        def to_mate(value):
            return lax.ppermute(value, 'cp', mate_perm)

        def to_cross(value):
            return lax.ppermute(value, 'cp', cross_perm)

        x_mate, dy_mate = to_mate(x_in), to_mate(grad_y)
        remote = []
        for seq in range(seqs):
            x_c, dy_c = to_cross(x_in[seq:seq + 1]), to_cross(grad_y[seq:seq + 1])
            remote.append((x_c, to_mate(x_c), dy_c, to_mate(dy_c)))

        exponent = jnp.arange(half, dtype=jnp.float32) * (1.0 / half)
        inv_freq = 1.0 / (long_factor * jnp.power(10000.0, exponent))
        all_pos = lax.all_gather(positions, 'cp', axis=0, tiled=True)
        angles = inv_freq[:, None] * all_pos.astype(jnp.float32)[None, :]
        cos, sin = jnp.cos(angles) * MSCALE, jnp.sin(angles) * MSCALE

        def rel_table(table, first, second):
            return jnp.concatenate([lax.dynamic_slice_in_dim(table, p * piece, piece, 1) for p in (first, second)], axis=1)[None]

        far, far_mate = lax.rem(me + 2, 4), lax.rem(mate + 2, 4)
        cos_loc, sin_loc = rel_table(cos, me, mate), rel_table(sin, me, mate)
        cos_rem, sin_rem = rel_table(cos, far, far_mate), rel_table(sin, far, far_mate)

        w_own = lax.dynamic_index_in_dim(w_qkv.reshape(hidden, 3, 2, part), core, 2, keepdims=False)
        w_cat = jnp.concatenate([jnp.transpose(w_own, (1, 2, 0)).reshape(3 * part, hidden),
                                 lax.dynamic_slice_in_dim(w_out, core * part, part, 0)], axis=0)
        gain = norm_gain[None, :]

        loc, r_loc, dyc_loc = project(w_cat, x_in, x_mate, grad_y, dy_mate, gain, cos_loc, sin_loc, head_dim)
        r_rems, dy_rems, grads, outs = [], [], [], []
        for seq in range(seqs):
            x_c, x_d, dy_c, dy_d = remote[seq]
            rem, r_rem, dyc_rem = project(w_cat, x_c, x_d, dy_c, dy_d, gain, cos_rem, sin_rem, head_dim)
            grad, out = attention(seq, loc, rem, cos, sin, head_dim)
            r_rems.append(r_rem)
            dy_rems.append(dyc_rem)
            grads.append(grad)
            outs.append(out)

        g_own = jnp.stack([g[0, :, :, :piece] for g in grads])
        g_mate = to_mate(jnp.stack([g[0, :, :, piece:] for g in grads]))
        o_own = jnp.stack([o[0, :, :piece] for o in outs])
        o_mate = to_mate(jnp.stack([o[0, :, piece:] for o in outs]))

        wout_own = grad_out(dyc_loc, dy_rems, outs)
        wout_mate = to_mate(wout_own)
        wqkv_own = [grad_qkv(r_loc, r_rems, grads, which) for which in range(3)]
        wqkv_mate = [to_mate(g) for g in wqkv_own]

        def both(own, other, axis):
            return jnp.concatenate([jnp.where(core == 0, own, other), jnp.where(core == 0, other, own)], axis=axis)

        w_out_own = lax.dynamic_slice_in_dim(w_out, core * part, part, 0)
        w_out_mate = lax.dynamic_slice_in_dim(w_out, (1 - core) * part, part, 0)
        w_mate = lax.dynamic_index_in_dim(w_qkv.reshape(hidden, 3, 2, part), 1 - core, 2, keepdims=False)

        x_float = x_in.astype(jnp.float32)
        proj = jnp.einsum('sht,hd->std', o_own, w_out_own, preferred_element_type=jnp.float32)
        proj = proj + jnp.einsum('sht,hd->std', o_mate, w_out_mate, preferred_element_type=jnp.float32)
        y_out = (x_float + proj).astype(jnp.bfloat16)

        inv_rms = lax.rsqrt(jnp.mean(x_float * x_float, axis=-1, keepdims=True) + NORM_EPS)
        x_hat = x_float * inv_rms
        d_normed = jnp.einsum('scht,dch->std', g_own, w_own, preferred_element_type=jnp.float32)
        d_normed = d_normed + jnp.einsum('scht,dch->std', g_mate, w_mate, preferred_element_type=jnp.float32)
        g_gain = lax.psum(jnp.sum(d_normed * x_hat, axis=(0, 1)), 'cp')
        d_hat = d_normed * norm_gain
        dx_norm = inv_rms * (d_hat - x_hat * jnp.mean(d_hat * x_hat, axis=-1, keepdims=True))
        grad_x = (grad_y.astype(jnp.float32) + dx_norm).astype(jnp.bfloat16)

        g_wqkv = jnp.concatenate([both(a, b, 1) for a, b in zip(wqkv_own, wqkv_mate)], axis=1)
        g_wout = both(wout_own, wout_mate, 0)
        return y_out, grad_x, g_gain, g_wqkv, g_wout

    seq_spec = P('dp', 'cp', None)
    return jax.shard_map(device_fn, mesh=mesh, in_specs=(seq_spec, P(('dp', 'cp')), P(None), P(None), P(None, None), P(None, None), seq_spec), out_specs=(seq_spec, seq_spec, P('dp'), P('dp', None), P('dp', None)), check_vma=False)
```

time: 3610 us -> 1070 us (0.30)
  waiting for transfers between devices: 2430 us -> 0.05 us
  Pallas kernels: 0 us -> 637 us
  starting transfers between devices: 489 us -> 10.6 us
  matrix products: 321 us -> 71.7 us
    ppermute x20, waiting for transfers between devices: 1410 us -> 0.05 us  [the longest x14 0.04 us: to_mate(): return lax.ppermute(value, 'cp', mate_perm)]
    psum x1 -> x0, waiting for transfers between devices: 1020 us -> none  [device_fn(): g_gain, g_wqkv, g_wout = lax.psum((g_gain, g_wqkv, g_wout), 'cp')]
    pallas_call x0 -> x11, Pallas kernels: none -> 637 us  [the longest x3 387 us: attention(): pl.pallas_call(functools.partial(attn_kernel, head_dim=head_dim, piece=pa...]
    ppermute x20, starting transfers between devices: 489 us -> 10.6 us  [the longest x6 7.44 us: to_cross(): return lax.ppermute(value, 'cp', cross_perm)]
    dot_general x12 -> x4, matrix products: 321 us -> 71.7 us  [the longest x1 26.1 us: device_fn(): jnp.einsum('scht,dch->std', g_mate, w_mate, preferred_element_type=jnp.fl...]
    while x18 -> x0, local copies, waits for them, and re-layouts: 111 us -> none
    unnamed x59 -> x27, local copies, waits for them, and re-layouts: 66.7 us -> 4.63 us
    dynamic_slice x0 -> x3, local copies, waits for them, and re-layouts: none -> 58.5 us  [the longest x1 55.9 us: device_fn(): lax.dynamic_index_in_dim(w_qkv.reshape(hidden, 3, 2, part), 1 - core, 2,...]
  transfers between devices with their start and end apart: 21 -> 20, of which waited for: 15 -> 0; matrix products, arithmetic and copies ran while one was open for 4% -> 31% of each run, Pallas kernels for 0% -> 12%
where the time goes in v1:
time: 1070 us; the launch traced here: 1060 us
  Pallas kernels  637 us (60%)
  local copies, waits for them, and re-layouts  199 us (19%)
  other arithmetic  107 us (10%)
  matrix products  71.7 us (7%)
  blocking collectives  30.9 us (3%)
    pallas_call x3, Pallas kernels, attention(): pl.pallas_call(functools.partial(attn_kernel, head_dim=head_dim, piece=pa...  387 us
    pallas_call x4, Pallas kernels, project(): pl.pallas_call(functools.partial(proj_kernel, head_dim=head_dim, row_bloc...  133 us
    pallas_call x3, Pallas kernels, grad_qkv(): pl.pallas_call(grad_qkv_kernel, grid=(part // bn, hidden // bm), in_specs...  85 us
    transpose x1, local copies, waits for them, and re-layouts, device_fn(): jnp.transpose(w_own, (1, 2, 0)).reshape(3 * part, hidden)  57.2 us
    dynamic_slice x1, local copies, waits for them, and re-layouts, device_fn(): lax.dynamic_index_in_dim(w_qkv.reshape(hidden, 3, 2, part), 1 - core, 2,...  55.9 us
    reshape x1, local copies, waits for them, and re-layouts, device_fn(): w_qkv.reshape(hidden, 3, 2, part)  53.2 us
    unnamed x5, other arithmetic  48.8 us
    pallas_call x1, Pallas kernels, grad_out(): pl.pallas_call(grad_out_kernel, grid=(hidden // bn, part // bm), in_specs...  31.6 us
  transfers between devices with their start and end apart: 20, of which 0 were waited for; matrix products, arithmetic and copies ran while one was open for 31% of the time, Pallas kernels for 12%

profile of v1, /device:TPU:0, one launch (start us, length us, event | category | flops | bytes accessed | tf_op | source)
XLA Modules:
  0.0 1057.7 jit_solution(15654276814420581115)
XLA Ops:
  0.6 4.9 fusion.38
  14.5 53.2 %reshape.32 = bf16[2048,3,2,1024]{3,2,1,0:T(2,128)(2,1)} reshape(bf16[2048,6144]{1,0:T(8,128)(2,1)} %param.11) | data formatting | bytes 50331648 | tf_op jit(solution)/shard_map/reshape | solution.py:290
  67.7 55.9 %constant_dynamic-slice_fusion = (bf16[2048,3,1,1024]{3,2,1,0:T(2,128)(2,1)}, bf16[2048,3,1,1024]{3,2,1,0:T(2,128)(2,1)}) fusion(bf16[2048,3,2,1024]{3,2,1,0:T(2,128)(2,1)} %reshape.32, s32[]{:T(128)S(6)} %select_n.77, s32[]{:T(128)S(6)} %select_n.70), kind=kLoop, calls=%fused_computation.57 | loop fusion | bytes 50331656 | tf_op jit(solution)/shard_map/jit(dynamic_index_in_dim)/dynamic_slice | solution.py:321
  123.6 57.2 %copy.34 = bf16[2048,3,1,1024]{0,3,1,2:T(8,128)(2,1)} copy(bf16[2048,3,1,1024]{3,2,1,0:T(2,128)(2,1)} %get-tuple-element.44) | data formatting | bytes 25165824 | tf_op jit(solution)/shard_map/transpose | solution.py:291
  185.4 12.3 %pad_maximum_fusion.w_ref = bf16[4096,2048]{1,0:T(8,128)(2,1)} fusion(bf16[1024,2048]{1,0:T(8,128)(2,1)S(1)} %constant_dynamic-slice_fusion.9, bf16[3072,2048]{1,0:T(8,128)(2,1)} %bitcast.42), kind=kLoop, calls=%fused_computation | loop fusion | flops 33554432 | bytes 33554432 | tf_op jit(solution)/shard_map/concatenate | solution.py:291
  197.7 22.4 %all-gather = s32[4,1,384]{2,1,0:T(1,128)S(1)} all-gather(s32[1,1,384]{2,1,0:T(1,128)S(1)} %reshape.34), channel_id=1, replica_groups=mesh['dp'=2,'cp'=4] {'cp'}, dimensions={0}, use_global_device_ids=true | all-gather | bytes 7680 | tf_op jit(solution)/shard_map/all_gather | solution.py:279
  229.2 23.3 %project.7 = (bf16[1,4096,768]{2,1,0:T(8,128)(2,1)}, bf16[1,768,2048]{2,1,0:T(8,128)(2,1)}, bf16[1,768,2048]{2,1,0:T(8,128)(2,1)}) custom-call(bf16[4096,2048]{1,0:T(8,128)(2,1)} %pad_maximum_fusion.w_ref, bf16[1,384,2048]{2,1,0:T(8,128)(2,1)} %collective-permute-done.10.xa_ref, bf16[1,384,2048]{2,1,0:T(8,128)(2,1)} %collective-permute-done.11.xb_ref, ...), custom_call_target="tpu_custom_call" | custom-call | flops 12884901888 | bytes 32505856 | tf_op jit(solution)/shard_map/project/pallas_call | solution.py:76
  253.6 22.7 %project.6 = (bf16[1,4096,768]{2,1,0:T(8,128)(2,1)}, bf16[1,768,2048]{2,1,0:T(8,128)(2,1)}, bf16[1,768,2048]{2,1,0:T(8,128)(2,1)}) custom-call(bf16[4096,2048]{1,0:T(8,128)(2,1)} %pad_maximum_fusion.w_ref, bf16[1,384,2048]{2,1,0:T(8,128)(2,1)} %collective-permute-done.6.xa_ref, bf16[1,384,2048]{2,1,0:T(8,128)(2,1)} %copy-done.11, ...), custom_call_target="tpu_custom_call" | custom-call | flops 12884901888 | bytes 32505856 | tf_op jit(solution)/shard_map/project/pallas_call | solution.py:76
  276.4 23.0 %project.5 = (bf16[1,4096,768]{2,1,0:T(8,128)(2,1)}, bf16[1,768,2048]{2,1,0:T(8,128)(2,1)}, bf16[1,768,2048]{2,1,0:T(8,128)(2,1)}) custom-call(bf16[4096,2048]{1,0:T(8,128)(2,1)} %pad_maximum_fusion.w_ref, bf16[1,384,2048]{2,1,0:T(8,128)(2,1)} %collective-permute-done.2.xa_ref, bf16[1,384,2048]{2,1,0:T(8,128)(2,1)} %collective-permute-done.3.xb_ref, ...), custom_call_target="tpu_custom_call" | custom-call | flops 12884901888 | bytes 32505856 | tf_op jit(solution)/shard_map/project/pallas_call | solution.py:76
  299.4 64.4 %project.4 = (bf16[3,4096,768]{2,1,0:T(8,128)(2,1)}, bf16[3,768,2048]{2,1,0:T(8,128)(2,1)}, bf16[3,768,2048]{2,1,0:T(8,128)(2,1)}) custom-call(bf16[4096,2048]{1,0:T(8,128)(2,1)} %pad_maximum_fusion.w_ref, bf16[3,384,2048]{2,1,0:T(8,128)(2,1)} %xa_ref.1, bf16[3,384,2048]{2,1,0:T(8,128)(2,1)} %collective-permute-done.xb_ref, bf16[3,384,2048]{2,1,0:T(8,128)(2,1)} %da_ref.1, ...), custom_call_target="tpu_custom_call" | custom-call | flops 38654705664 | bytes 63963136 | tf_op jit(solution)/shard_map/project/pallas_call | solution.py:76
  363.8 128.9 %attention.5 = (bf16[2,3,1024,768]{3,2,1,0:T(8,128)(2,1)}, bf16[2,1024,768]{2,1,0:T(8,128)(2,1)}) custom-call(bf16[3,4096,768]{2,1,0:T(8,128)(2,1)} %get-tuple-element.23.refs_0_.refs_1_.refs_2_.refs_3_, bf16[3,4096,768]{2,1,0:T(8,128)(2,1)} %get-tuple-element.23.refs_0_.refs_1_.refs_2_.refs_3_, ...), custom_call_target="tpu_custom_call" | custom-call | flops 57982058496 | bytes 25165824 | tf_op jit(solution)/shard_map/attention/pallas_call | solution.py:176
  492.7 5.0 fusion.37
  497.8 129.3 %attention.4 = (bf16[2,3,1024,768]{3,2,1,0:T(8,128)(2,1)}, bf16[2,1024,768]{2,1,0:T(8,128)(2,1)}) custom-call(bf16[3,4096,768]{2,1,0:T(8,128)(2,1)} %get-tuple-element.23.refs_0_.refs_1_.refs_2_.refs_3_, bf16[3,4096,768]{2,1,0:T(8,128)(2,1)} %get-tuple-element.23.refs_0_.refs_1_.refs_2_.refs_3_, ...), custom_call_target="tpu_custom_call" | custom-call | flops 57982058496 | bytes 25165824 | tf_op jit(solution)/shard_map/attention/pallas_call | solution.py:176
  627.1 129.1 %attention.3 = (bf16[2,3,1024,768]{3,2,1,0:T(8,128)(2,1)}, bf16[2,1024,768]{2,1,0:T(8,128)(2,1)}) custom-call(bf16[3,4096,768]{2,1,0:T(8,128)(2,1)} %get-tuple-element.23.refs_0_.refs_1_.refs_2_.refs_3_, bf16[3,4096,768]{2,1,0:T(8,128)(2,1)} %get-tuple-element.23.refs_0_.refs_1_.refs_2_.refs_3_, ...), custom_call_target="tpu_custom_call" | custom-call | flops 57982058496 | bytes 25165824 | tf_op jit(solution)/shard_map/attention/pallas_call | solution.py:176
  764.9 28.1 %grad_qkv.3 = f32[2048,1024]{1,0:T(8,128)} custom-call(bf16[3,768,2048]{2,1,0:T(8,128)(2,1)} %get-tuple-element.33.refs_0_, bf16[1,768,2048]{2,1,0:T(8,128)(2,1)} %get-tuple-element.34.refs_1_, bf16[1,768,2048]{2,1,0:T(8,128)(2,1)} %get-tuple-element.35.refs_2_, bf16[1,768,2048]{2,1,0:T(8,128)(2,1)} %get-tuple-element.36.refs_3_, ...), custom_call_target="tpu_custom_call" | custom-call | flops 19327352832 | bytes 36700160 | tf_op jit(solution)/shard_map/grad_qkv/pallas_call | solution.py:209
  793.0 28.2 %grad_qkv.5 = f32[2048,1024]{1,0:T(8,128)} custom-call(bf16[3,768,2048]{2,1,0:T(8,128)(2,1)} %get-tuple-element.33.refs_0_, bf16[1,768,2048]{2,1,0:T(8,128)(2,1)} %get-tuple-element.34.refs_1_, bf16[1,768,2048]{2,1,0:T(8,128)(2,1)} %get-tuple-element.35.refs_2_, bf16[1,768,2048]{2,1,0:T(8,128)(2,1)} %get-tuple-element.36.refs_3_, ...), custom_call_target="tpu_custom_call" | custom-call | flops 19327352832 | bytes 36700160 | tf_op jit(solution)/shard_map/grad_qkv/pallas_call | solution.py:209
  834.2 31.6 %grad_out.1 = f32[1024,2048]{1,0:T(8,128)} custom-call(bf16[3,768,2048]{2,1,0:T(8,128)(2,1)} %get-tuple-element.37.refs_0_, bf16[1,768,2048]{2,1,0:T(8,128)(2,1)} %get-tuple-element.38.refs_1_, bf16[1,768,2048]{2,1,0:T(8,128)(2,1)} %get-tuple-element.39.refs_2_, bf16[1,768,2048]{2,1,0:T(8,128)(2,1)} %get-tuple-element.40.refs_3_, ...), custom_call_target="tpu_custom_call" | custom-call | flops 19327352832 | bytes 36700160 | tf_op jit(solution)/shard_map/grad_out/pallas_call | solution.py:238
  866.1 24.0 %fusion.4 = f32[3,384,2048,1]{2,1,3,0:T(8,128)} fusion(bf16[2048,3,1,1024]{3,2,1,0:T(2,128)(2,1)} %get-tuple-element.44, bf16[1,3,1024,384]{3,2,1,0:T(8,128)(2,1)S(1)} %copy-done.5, bf16[1,3,1024,384]{3,2,1,0:T(8,128)(2,1)} %get-tuple-element.50, bf16[1,3,1024,384]{3,2,1,0:T(8,128)(2,1)} %get-tuple-element.48), kind=kOutput, calls=%fused_computation.11 | convolution fusion | flops 14502592512 | bytes 29097984 | tf_op jit(solution)/shard_map/scht,dch->std/dot_general | solution.py:330
  890.2 9.6 fusion.20
  899.7 28.7 %grad_qkv.4 = f32[2048,1024]{1,0:T(8,128)} custom-call(bf16[3,768,2048]{2,1,0:T(8,128)(2,1)} %get-tuple-element.33.refs_0_, bf16[1,768,2048]{2,1,0:T(8,128)(2,1)} %get-tuple-element.34.refs_1_, bf16[1,768,2048]{2,1,0:T(8,128)(2,1)} %get-tuple-element.35.refs_2_, bf16[1,768,2048]{2,1,0:T(8,128)(2,1)} %get-tuple-element.36.refs_3_, ...), custom_call_target="tpu_custom_call" | custom-call | flops 19327352832 | bytes 36700160 | tf_op jit(solution)/shard_map/grad_qkv/pallas_call | solution.py:209
  928.6 12.0 %fusion.11 = bf16[3,384,2048]{2,1,0:T(8,128)(2,1)} fusion(bf16[3,384,2048]{2,1,0:T(8,128)(2,1)} %xa_ref.1, f32[3,384,2048]{2,1,0:T(8,128)} %fusion.20, bf16[3,1024,384]{2,1,0:T(8,128)(2,1)} %collective-permute-done.14, bf16[2048,2048]{1,0:T(8,128)(2,1)} %param.12, s32[]{:T(128)S(6)} %select_n.76), kind=kOutput, calls=%fused_computation.18 | convolution fusion | flops 4841275392 | bytes 25427972 | tf_op jit(solution)/shard_map/sht,hd->std/dot_general | solution.py:325
  940.6 26.1 %fusion.10 = (f32[2048]{0:T(1024)S(1)}, f32[3,384]{1,0:T(4,128)S(1)}, f32[3,384,2048]{2,1,0:T(8,128)}) fusion(bf16[3,384,2048]{2,1,0:T(8,128)(2,1)} %xa_ref.1, f32[3,384]{1,0:T(4,128)S(1)} %copy-done.8, f32[2048]{0:T(1024)S(1)} %copy-done.9, bf16[3,3,1024,384]{3,2,1,0:T(8,128)(2,1)} %collective-permute-done.15, ...), kind=kOutput, calls=%fused_computation.17 | convolution fusion | flops 14514385920 | bytes 43279360 | tf_op jit(solution)/shard_map/scht,dch->std/dot_general | solution.py:331
  966.7 8.6 psum.7
  975.3 10.3 fusion.9
  985.5 6.7 broadcast_select_fusion.1
  992.3 6.6 pad_maximum_fusion.1
  998.9 9.8 select_dynamic-update-slice_fusion.5
  1008.7 9.8 select_dynamic-update-slice_fusion.4
  1018.5 9.8 select_dynamic-update-slice_fusion.3
  1028.2 9.8 select_dynamic-update-slice_fusion.2
  1038.0 9.8 select_dynamic-update-slice_fusion.1
  1047.8 9.8 select_dynamic-update-slice_fusion
  (88 shorter events, 45.9 us)
Async XLA Ops:
  0.6 10.2 copy-start
  5.5 177.9 %collective-permute-start.4 = (bf16[1,384,2048]{2,1,0:T(8,128)(2,1)}, bf16[1,384,2048]{2,1,0:T(8,128)(2,1)}, u32[]{:S(2)}, u32[]{:S(2)}) collective-permute-start(bf16[1,384,2048]{2,1,0:T(8,128)(2,1)} %get-tuple-element.53), channel_id=1, source_target_pairs={{0,2},{1,3},{2,0},{3,1},{4,6},{5,7},{6,4},{7,5}} | collective-permute-start | bytes 4718600 | tf_op jit(solution)/shard_map/ppermute | solution.py:269
  8.8 174.6 %collective-permute-start.8 = (bf16[1,384,2048]{2,1,0:T(8,128)(2,1)}, bf16[1,384,2048]{2,1,0:T(8,128)(2,1)}, u32[]{:S(2)}, u32[]{:S(2)}) collective-permute-start(bf16[1,384,2048]{2,1,0:T(8,128)(2,1)} %get-tuple-element.54), channel_id=1, source_target_pairs={{0,2},{1,3},{2,0},{3,1},{4,6},{5,7},{6,4},{7,5}} | collective-permute-start | bytes 4718600 | tf_op jit(solution)/shard_map/ppermute | solution.py:269
  8.9 211.3 %collective-permute-start.12 = (bf16[1,384,2048]{2,1,0:T(8,128)(2,1)}, bf16[1,384,2048]{2,1,0:T(8,128)(2,1)}, u32[]{:S(2)}, u32[]{:S(2)}) collective-permute-start(bf16[1,384,2048]{2,1,0:T(8,128)(2,1)} %get-tuple-element.55), channel_id=1, source_target_pairs={{0,2},{1,3},{2,0},{3,1},{4,6},{5,7},{6,4},{7,5}} | collective-permute-start | bytes 4718600 | tf_op jit(solution)/shard_map/ppermute | solution.py:269
  12.5 209.0 %collective-permute-start.2 = (bf16[1,384,2048]{2,1,0:T(8,128)(2,1)S(1)}, bf16[1,384,2048]{2,1,0:T(8,128)(2,1)}, u32[]{:S(2)}, u32[]{:S(2)}) collective-permute-start(bf16[1,384,2048]{2,1,0:T(8,128)(2,1)S(1)} %get-tuple-element.56), channel_id=1, source_target_pairs={{0,2},{1,3},{2,0},{3,1},{4,6},{5,7},{6,4},{7,5}} | collective-permute-start | bytes 4718600 | tf_op jit(solution)/shard_map/ppermute | solution.py:269
  12.5 207.7 %collective-permute-start.10 = (bf16[1,384,2048]{2,1,0:T(8,128)(2,1)}, bf16[1,384,2048]{2,1,0:T(8,128)(2,1)}, u32[]{:S(2)}, u32[]{:S(2)}) collective-permute-start(bf16[1,384,2048]{2,1,0:T(8,128)(2,1)} %get-tuple-element.57), channel_id=1, source_target_pairs={{0,2},{1,3},{2,0},{3,1},{4,6},{5,7},{6,4},{7,5}} | collective-permute-start | bytes 4718600 | tf_op jit(solution)/shard_map/ppermute | solution.py:269
  183.4 2.0 copy-start.1
  183.4 38.2 %collective-permute-start.6 = (bf16[1,384,2048]{2,1,0:T(8,128)(2,1)S(1)}, bf16[1,384,2048]{2,1,0:T(8,128)(2,1)}, u32[]{:S(2)}, u32[]{:S(2)}) collective-permute-start(bf16[1,384,2048]{2,1,0:T(8,128)(2,1)S(1)} %get-tuple-element.58), channel_id=1, source_target_pairs={{0,2},{1,3},{2,0},{3,1},{4,6},{5,7},{6,4},{7,5}} | collective-permute-start | bytes 4718600 | tf_op jit(solution)/shard_map/ppermute | solution.py:269
  183.4 43.3 %collective-permute-start.9 = (bf16[1,384,2048]{2,1,0:T(8,128)(2,1)}, bf16[1,384,2048]{2,1,0:T(8,128)(2,1)}, u32[]{:S(2)}, u32[]{:S(2)}) collective-permute-start(bf16[1,384,2048]{2,1,0:T(8,128)(2,1)} %collective-permute-done.8.da_ref), channel_id=1, source_target_pairs={{0,1},{1,0},{2,3},{3,2},{4,5},{5,4},{6,7},{7,6}} | collective-permute-start | bytes 4718600 | tf_op jit(solution)/shard_map/ppermute | solution.py:266
  185.4 12.3 %copy-start.10 = (s32[384]{0:T(512)S(1)}, s32[384]{0:T(512)}, u32[]{:S(2)}) copy-start(s32[384]{0:T(512)} %param.8) | copy-start | bytes 4612
  185.4 34.8 %copy-start.12 = (f32[32]{0:T(128)S(1)}, f32[32]{0:T(128)}, u32[]{:S(2)}) copy-start(f32[32]{0:T(128)} %param.9) | copy-start | bytes 388
  220.2 8.5 collective-permute-start.13
  220.2 8.9 collective-permute-start.11
  221.5 31.0 %copy-start.6 = (f32[32,1536]{1,0:T(8,128)}, f32[32,1536]{1,0:T(8,128)S(1)}, u32[]{:S(2)}) copy-start(f32[32,1536]{1,0:T(8,128)S(1)} %get-tuple-element.73.refs_9_) | copy-start | bytes 589828
  221.5 31.0 %copy-start.7 = (f32[32,1536]{1,0:T(8,128)}, f32[32,1536]{1,0:T(8,128)S(1)}, u32[]{:S(2)}) copy-start(f32[32,1536]{1,0:T(8,128)S(1)} %get-tuple-element.74.refs_8_) | copy-start | bytes 589828
  221.5 77.9 %collective-permute-start.1 = (bf16[3,384,2048]{2,1,0:T(8,128)(2,1)}, bf16[3,384,2048]{2,1,0:T(8,128)(2,1)}, u32[]{:S(2)}, u32[]{:S(2)}) collective-permute-start(bf16[3,384,2048]{2,1,0:T(8,128)(2,1)} %da_ref.1), channel_id=1, source_target_pairs={{0,1},{1,0},{2,3},{3,2},{4,5},{5,4},{6,7},{7,6}} | collective-permute-start | bytes 14155784 | tf_op jit(solution)/shard_map/ppermute | solution.py:266
  221.6 77.9 %collective-permute-start = (bf16[3,384,2048]{2,1,0:T(8,128)(2,1)}, bf16[3,384,2048]{2,1,0:T(8,128)(2,1)}, u32[]{:S(2)}, u32[]{:S(2)}) collective-permute-start(bf16[3,384,2048]{2,1,0:T(8,128)(2,1)} %xa_ref.1), channel_id=1, source_target_pairs={{0,1},{1,0},{2,3},{3,2},{4,5},{5,4},{6,7},{7,6}} | collective-permute-start | bytes 14155784 | tf_op jit(solution)/shard_map/ppermute | solution.py:266
  226.7 25.8 %collective-permute-start.7 = (bf16[1,384,2048]{2,1,0:T(8,128)(2,1)}, bf16[1,384,2048]{2,1,0:T(8,128)(2,1)S(1)}, u32[]{:S(2)}, u32[]{:S(2)}) collective-permute-start(bf16[1,384,2048]{2,1,0:T(8,128)(2,1)} %collective-permute-done.6.xa_ref), channel_id=1, source_target_pairs={{0,1},{1,0},{2,3},{3,2},{4,5},{5,4},{6,7},{7,6}} | collective-permute-start | bytes 4718600 | tf_op jit(solution)/shard_map/ppermute | solution.py:266
  228.7 47.7 %collective-permute-start.5 = (bf16[1,384,2048]{2,1,0:T(8,128)(2,1)}, bf16[1,384,2048]{2,1,0:T(8,128)(2,1)}, u32[]{:S(2)}, u32[]{:S(2)}) collective-permute-start(bf16[1,384,2048]{2,1,0:T(8,128)(2,1)} %collective-permute-done.4.da_ref), channel_id=1, source_target_pairs={{0,1},{1,0},{2,3},{3,2},{4,5},{5,4},{6,7},{7,6}} | collective-permute-start | bytes 4718600 | tf_op jit(solution)/shard_map/ppermute | solution.py:266
  229.2 47.2 %collective-permute-start.3 = (bf16[1,384,2048]{2,1,0:T(8,128)(2,1)}, bf16[1,384,2048]{2,1,0:T(8,128)(2,1)}, u32[]{:S(2)}, u32[]{:S(2)}) collective-permute-start(bf16[1,384,2048]{2,1,0:T(8,128)(2,1)} %collective-permute-done.2.xa_ref), channel_id=1, source_target_pairs={{0,1},{1,0},{2,3},{3,2},{4,5},{5,4},{6,7},{7,6}} | collective-permute-start | bytes 4718600 | tf_op jit(solution)/shard_map/ppermute | solution.py:266
  756.2 6.0 copy-start.4
  821.2 8.8 copy-start.2
  821.2 8.8 copy-start.3
  829.6 98.8 %collective-permute-start.14 = (bf16[3,1024,384]{2,1,0:T(8,128)(2,1)}, bf16[3,1024,384]{2,1,0:T(8,128)(2,1)}, u32[]{:S(2)}, u32[]{:S(2)}) collective-permute-start(bf16[3,1024,384]{2,1,0:T(8,128)(2,1)} %pad_maximum_fusion.3), channel_id=1, source_target_pairs={{0,1},{1,0},{2,3},{3,2},{4,5},{5,4},{6,7},{7,6}} | collective-permute-start | bytes 7077896 | tf_op jit(solution)/shard_map/ppermute | solution.py:266
  833.5 107.1 %collective-permute-start.15 = (bf16[3,3,1024,384]{3,2,1,0:T(8,128)(2,1)}, bf16[3,3,1024,384]{3,2,1,0:T(8,128)(2,1)}, u32[]{:S(2)}, u32[]{:S(2)}) collective-permute-start(bf16[3,3,1024,384]{3,2,1,0:T(8,128)(2,1)} %pad_maximum_fusion.2), channel_id=1, source_target_pairs={{0,1},{1,0},{2,3},{3,2},{4,5},{5,4},{6,7},{7,6}} | collective-permute-start | bytes 21233672 | tf_op jit(solution)/shard_map/ppermute | solution.py:266
  833.7 204.3 %collective-permute-start.18 = (f32[2048,1024]{1,0:T(8,128)}, f32[2048,1024]{1,0:T(8,128)}, u32[]{:S(2)}, u32[]{:S(2)}) collective-permute-start(f32[2048,1024]{1,0:T(8,128)} %grad_qkv.5), channel_id=1, source_target_pairs={{0,1},{1,0},{2,3},{3,2},{4,5},{5,4},{6,7},{7,6}} | collective-permute-start | bytes 25165832 | tf_op jit(solution)/shard_map/ppermute | solution.py:266
  834.0 164.9 %collective-permute-start.16 = (f32[2048,1024]{1,0:T(8,128)}, f32[2048,1024]{1,0:T(8,128)}, u32[]{:S(2)}, u32[]{:S(2)}) collective-permute-start(f32[2048,1024]{1,0:T(8,128)} %grad_qkv.3), channel_id=1, source_target_pairs={{0,1},{1,0},{2,3},{3,2},{4,5},{5,4},{6,7},{7,6}} | collective-permute-start | bytes 25165832 | tf_op jit(solution)/shard_map/ppermute | solution.py:266
  834.2 31.9 %copy-start.5 = (bf16[1,3,1024,384]{3,2,1,0:T(8,128)(2,1)S(1)}, bf16[1,3,1024,384]{3,2,1,0:T(8,128)(2,1)}, u32[]{:S(2)}) copy-start(bf16[1,3,1024,384]{3,2,1,0:T(8,128)(2,1)} %get-tuple-element.52) | copy-start | bytes 7077892
  865.8 119.7 %collective-permute-start.19 = (f32[1024,2048]{1,0:T(8,128)}, f32[1024,2048]{1,0:T(8,128)}, u32[]{:S(2)}, u32[]{:S(2)}) collective-permute-start(f32[1024,2048]{1,0:T(8,128)} %grad_out.1), channel_id=1, source_target_pairs={{0,1},{1,0},{2,3},{3,2},{4,5},{5,4},{6,7},{7,6}} | collective-permute-start | bytes 25165832 | tf_op jit(solution)/shard_map/ppermute | solution.py:266
  928.4 12.2 %copy-start.8 = (f32[3,384]{1,0:T(4,128)S(1)}, f32[3,384]{1,0:T(4,128)}, u32[]{:S(2)}) copy-start(f32[3,384]{1,0:T(4,128)} %add_rsqrt_fusion) | copy-start | bytes 13828
  928.4 12.2 %copy-start.9 = (f32[2048]{0:T(1024)S(1)}, f32[2048]{0:T(1024)}, u32[]{:S(2)}) copy-start(f32[2048]{0:T(1024)} %param.10) | copy-start | bytes 24580
  928.4 90.1 %collective-permute-start.17 = (f32[2048,1024]{1,0:T(8,128)}, f32[2048,1024]{1,0:T(8,128)}, u32[]{:S(2)}, u32[]{:S(2)}) collective-permute-start(f32[2048,1024]{1,0:T(8,128)} %grad_qkv.4), channel_id=1, source_target_pairs={{0,1},{1,0},{2,3},{3,2},{4,5},{5,4},{6,7},{7,6}} | collective-permute-start | bytes 25165832 | tf_op jit(solution)/shard_map/ppermute | solution.py:266
  (1 other events, 1.1 us)
